TPU v7x, 256 devices: a whole 4x4x8 slice. The times are simulated.
256 devices in a mesh: src: 32 (over y_lo, z, core), tgt: 8 (over x, y_hi).
Axes of the slice: x: 4, y: 4 (y_hi: 2, y_lo: 2; y = y_hi * 2 + y_lo), z: 8, core: 2. Of those that a mesh axis runs over, the one named last changes fastest.
Arguments:
- atom_feats: bfloat16 [2048, 3200], P(('src', 'tgt')), may hold values from -6 to 6
- positions: float32 [3, 2048], P(None, ('src', 'tgt')), may hold values from 0 to 1
- edge_src: int32 [262144], P(('src', 'tgt')), may hold values from 0 to 63
- edge_tgt: int32 [262144], P(('src', 'tgt')), may hold values from 0 to 255
- edge_angle: float32 [262144], P(('src', 'tgt')), may hold values from -3.140625 to 3.140625
- edge_scale: float32 [262144], P(('src', 'tgt')), may hold values from 0.1 to 1
- edge_count: int32 [32, 8], replicated, may hold values from 1 to 1024, as said below
- k_index: int32 [3, 2048], replicated, may hold values from -6 to 6
- k_filter: float32 [2048, 128], replicated, may hold values from -6 to 6
- weight_zero: bfloat16 [2, 640, 640], replicated, may hold values from -0.25 to 0.25
- weight_first: bfloat16 [2, 2, 512, 512], replicated, may hold values from -0.1875 to 0.1875
- weight_second: bfloat16 [2, 2, 384, 384], replicated, may hold values from -0.21875 to 0.21875
- weight_third: bfloat16 [2, 2, 256, 256], replicated, may hold values from -0.25 to 0.25
- weight_fourth: bfloat16 [2, 2, 128, 128], replicated, may hold values from -0.375 to 0.375
Outputs:
- edge_update: bfloat16 [2048, 3200], P(('tgt', 'src'))
- long_range: float32 [2048, 128], P(('src', 'tgt'))
Inputs may be any that keep to these rules, and one draw needn't show every extreme that they name: `edge_count`: live edge slots of tile (s, t); in every draw some tile is full with 1024.
All inputs are finite; a program needn't handle non-finite values.
Results may differ from a plain program's by a relative error of at most 0.0047.
Values may be sent and summed in bfloat16 or wider, within the bound.
No kernel may reach another device: no remote copies, remote signals or barrier semaphores. Data moves between devices by JAX's collectives and lax.ppermute only.
A program may use at most 64 MiB of HBM per device.

v0:
```python
import math
import jax
import jax.numpy as jnp
from jax import lax
from jax.sharding import PartitionSpec as P


def rotate(values, angles, handed, channels, degrees):
    pieces = [values[:, : (degrees + 1) * channels]]
    offset = (degrees + 1) * channels
    for degree in range(1, degrees + 1):
        columns = (degrees + 1 - degree) * channels
        cosine = jnp.cos(degree * angles)[:, None]
        sine_part = handed * jnp.sin(degree * angles)[:, None]
        leading = values[:, offset : offset + columns]
        trailing = values[:, offset + columns : offset + 2 * columns]
        pieces.append(cosine * leading + sine_part * trailing)
        pieces.append(cosine * trailing - sine_part * leading)
        offset += 2 * columns
    return jnp.concatenate(pieces, axis=1)


def pair_matrix(weights, conv_index):
    upper_half = jnp.concatenate([weights[conv_index, 0], weights[conv_index, 1]], axis=1)
    lower_half = jnp.concatenate([-weights[conv_index, 1], weights[conv_index, 0]], axis=1)
    return jnp.concatenate([upper_half, lower_half], axis=0)


def convolve(inputs, matrices):
    outputs = []
    offset = 0
    for matrix in matrices:
        height = matrix.shape[0]
        outputs.append(
            jnp.dot(inputs[:, offset : offset + height], matrix, preferred_element_type=jnp.float32)
        )
        offset += height
    return jnp.concatenate(outputs, axis=1)


def phase_table(coords, k_index):
    k_float = k_index.astype(jnp.float32)
    return (
        2.0
        * math.pi
        * (
            coords[0][:, None] * k_float[0][None, :]
            + coords[1][:, None] * k_float[1][None, :]
            + coords[2][:, None] * k_float[2][None, :]
        )
    )


def highest_dot(left_side, right_side):
    return jnp.dot(
        left_side, right_side, precision=lax.Precision.HIGHEST, preferred_element_type=jnp.float32
    )


def body(
    atom_feats,
    positions,
    edge_src,
    edge_tgt,
    edge_angle,
    edge_scale,
    edge_count,
    k_index,
    k_filter,
    weight_zero,
    weight_first,
    weight_second,
    weight_third,
    weight_fourth,
):
    channels = k_filter.shape[1]
    degrees = 4
    capacity = edge_src.shape[0]
    source_count = lax.axis_size("src")
    target_count = lax.axis_size("tgt")
    own_atoms = atom_feats.shape[0]
    target_rows = own_atoms * source_count
    feat_columns = atom_feats.shape[1]
    source_group = lax.axis_index("src")
    target_group = lax.axis_index("tgt")
    sections = []
    for conv_index in (0, 1):
        sections.append(
            [weight_zero[conv_index]]
            + [
                pair_matrix(weights, conv_index)
                for weights in (weight_first, weight_second, weight_third, weight_fourth)
            ]
        )
    block_feats = lax.all_gather(atom_feats, "tgt", axis=0, tiled=True)
    step_rows = math.gcd(256, capacity // 2)
    lane_ids = jnp.arange(step_rows, dtype=jnp.int32)
    target_ids = jnp.arange(target_rows, dtype=jnp.int32)

    def edge_message(edge_rows, angles, scales):
        turned = rotate(edge_rows.astype(jnp.float32), angles, 1.0, channels, degrees).astype(
            jnp.bfloat16
        )
        hidden = jax.nn.gelu(convolve(turned, sections[0]), approximate=False).astype(jnp.bfloat16)
        second = convolve(hidden, sections[1])
        return rotate(second, angles, -1.0, channels, degrees) * scales[:, None]

    def own_rows(first_slot):
        return jnp.take(
            block_feats, lax.dynamic_slice_in_dim(edge_src, first_slot, step_rows), axis=0
        )

    count_here = edge_count[source_group, target_group]
    zeros_total = jnp.zeros((target_rows, feat_columns), jnp.float32)

    def one_block(block_number, carried):
        first_slot = block_number * step_rows
        edge_rows = own_rows(first_slot)
        angles = lax.dynamic_slice_in_dim(edge_angle, first_slot, step_rows)
        scales = lax.dynamic_slice_in_dim(edge_scale, first_slot, step_rows)
        targets = lax.dynamic_slice_in_dim(edge_tgt, first_slot, step_rows)
        slot_ids = first_slot + lane_ids
        live_mask = ((slot_ids >= 0) & (slot_ids < count_here)).astype(jnp.float32)
        messages = edge_message(edge_rows, angles, scales) * live_mask[:, None]
        one_hot = (targets[:, None] == target_ids[None, :]).astype(jnp.float32)
        added = lax.dot_general(
            one_hot,
            messages,
            (((0,), (0,)), ((), ())),
            precision=lax.Precision.HIGHEST,
            preferred_element_type=jnp.float32,
        )
        return carried + added

    totals = lax.fori_loop(0, (count_here + step_rows - 1) // step_rows, one_block, zeros_total)
    edge_update = lax.psum_scatter(totals, "src", scatter_dimension=0, tiled=True).astype(
        jnp.bfloat16
    )
    total_atoms = own_atoms * source_count * target_count
    norm_factor = 1.0 / math.sqrt(total_atoms * k_filter.shape[0])
    phase = phase_table(positions, k_index)
    cos_table = jnp.cos(phase)
    sin_table = jnp.sin(phase)
    charges = atom_feats[:, :channels].astype(jnp.float32)
    factors_cos, factors_sin = lax.psum(
        (highest_dot(cos_table.T, charges), highest_dot(sin_table.T, charges)), ("src", "tgt")
    )
    summed = highest_dot(cos_table, k_filter * factors_cos) + highest_dot(
        sin_table, k_filter * factors_sin
    )
    long_range = summed * norm_factor
    return (edge_update, long_range)


def solution(mesh):
    return jax.shard_map(
        body,
        mesh=mesh,
        in_specs=(
            P(("src", "tgt"), None),
            P(None, ("src", "tgt")),
            P(("src", "tgt")),
            P(("src", "tgt")),
            P(("src", "tgt")),
            P(("src", "tgt")),
            P(),
            P(),
            P(),
            P(),
            P(),
            P(),
            P(),
            P(),
        ),
        out_specs=(P(("tgt", "src"), None), P(("src", "tgt"), None)),
        check_vma=False,
    )
```

profile of v0, /device:TPU:8, one launch (start us, length us, event | category | flops | bytes accessed | tf_op | source)
XLA Modules:
  0.0 330.4 jit_solution(7613350348428769478)
XLA Ops:
  7.2 0.8 slice_bitcast_fusion.20
  8.0 0.8 convert_element_type.28
  8.8 2.9 fusion.53
  11.8 2.9 fusion.50
  14.7 1.5 dynamic_slice.19
  17.6 34.9 %all_gather.3 = bf16[64,3200]{1,0:T(8,128)(2,1)S(1)} all-gather(bf16[8,3200]{1,0:T(8,128)(2,1)S(1)} %copy-done.29), channel_id=1, replica_groups=mesh['src'=32,'tgt'=8] {'tgt'}, dimensions={0}, use_global_device_ids=true | all-gather | bytes 460800 | tf_op jit(solution)/shard_map/all_gather | solution.py:95
  53.1 0.8 slice_bitcast_fusion.10
  53.9 1.9 fusion.94
  55.9 2.3 slice_bitcast_fusion.6
  58.2 0.9 fusion.96
  59.0 1.4 slice_bitcast_fusion.2
  60.5 2.8 slice_bitcast_fusion
  63.4 1.1 maximum_maximum_fusion.4
  64.5 2.8 maximum_maximum_fusion.2
  67.3 5.8 %maximum_maximum_fusion = (bf16[1024,1024]{1,0:T(8,128)(2,1)}, bf16[1024,1024]{1,0:T(8,128)(2,1)}) fusion(bf16[512,512]{1,0:T(8,128)(2,1)} %get-tuple-element.309, bf16[512,512]{1,0:T(8,128)(2,1)S(1)} %copy-done.10, bf16[512,512]{1,0:T(8,128)(2,1)} %get-tuple-element.308, bf16[512,512]{1,0:T(8,128)(2,1)} %get-tuple-element.310, ...), kind=kLoop, calls=%fused_computation.92 | loop fusion | flops 16777216 | bytes 7340032 | tf_op jit(solution)/shard_map/concatenate | solution.py:26
  73.1 1.9 broadcast.175
  75.0 29.6 %while.13 = (s32[]{:T(128)}, f32[256,3200]{1,0:T(8,128)}, s32[]{:T(128)}, s32[1024]{0:T(1024)}, s32[1024]{0:T(1024)}, /*index=5*/bf16[64,3200]{1,0:T(8,128)(2,1)...) while((s32[]{:T(128)}, f32[256,3200]{1,0:T(8,128)}, ...), condition=%wide.region_1.2_spmd.clone.clone, body=%wide.region_0.1_spmd.clone.clone.sunk | while | flops 5013903360 | bytes 114246840 | solution.py:135
  75.0 1.3 dynamic_slice.35
  76.3 1.3 dynamic_slice.36
  77.6 2.0 compare_and_fusion.2
  79.6 0.8 broadcast_multiply_fusion.7
  81.1 1.8 gather_fusion
  82.9 1.1 fusion.157
  85.8 0.7 convolution_dynamic-update-slice_fusion.13
  87.6 7.2 %fusion.158 = bf16[256,3200]{1,0:T(8,128)(2,1)S(1)} fusion(f32[256,3200]{1,0:T(8,128)S(1)} %convolution_dynamic-update-slice_fusion.16), kind=kLoop, calls=%fused_computation.6.clone.1 | loop fusion | flops 53248000 | bytes 4915200 | tf_op jit(solution)/shard_map/while/body/convert_element_type | solution.py:104
  96.4 0.7 fusion.159
  98.7 0.9 copy-done
  99.6 3.3 convolution_add_fusion.3
  102.9 1.7 copy-done.1
  104.6 212.1 %all-reduce.6 = bf16[256,3200]{1,0:T(8,128)(2,1)S(1)} all-reduce(f32[256,3200]{1,0:T(8,128)} %get-tuple-element.155), channel_id=2, replica_groups=mesh['src'=32,'tgt'=8] {'src'}, use_global_device_ids=true, to_apply=%region_2.3.clone | all-reduce | flops 819200 | bytes 4915200
  318.6 2.1 fusion.45
  320.8 2.8 fusion.43
  (105 shorter events, 9.3 us)
Async XLA Ops:
  7.2 10.4 %copy-start.29 = (bf16[8,3200]{1,0:T(8,128)(2,1)S(1)}, bf16[8,3200]{1,0:T(8,128)(2,1)}, u32[]{:S(2)}) copy-start(bf16[8,3200]{1,0:T(8,128)(2,1)} %param.16) | copy-start | bytes 153604
  7.2 9.7 %copy-start.19 = (bf16[2,2,128,128]{3,2,1,0:T(8,128)(2,1)S(1)}, bf16[2,2,128,128]{3,2,1,0:T(8,128)(2,1)}, u32[]{:S(2)}) copy-start(bf16[2,2,128,128]{3,2,1,0:T(8,128)(2,1)} %param.29) | copy-start | bytes 393220
  7.2 45.3 %copy-start.13 = (bf16[2,2,256,256]{3,2,1,0:T(8,128)(2,1)S(1)}, bf16[2,2,256,256]{3,2,1,0:T(8,128)(2,1)}, u32[]{:S(2)}) copy-start(bf16[2,2,256,256]{3,2,1,0:T(8,128)(2,1)} %param.28) | copy-start | bytes 1572868
  7.2 311.4 %all-reduce.5.cloned.1.call-start = ((), (), s32[]{:S(2)}) async-start(), calls=%async_computation | async-start | bytes 4194304 | tf_op jit(solution)/shard_map/psum | solution.py:145
  8.0 8.8 %copy-start.30 = (f32[8]{0:T(128)}, f32[8]{0:T(128)S(1)}, u32[]{:S(2)}) copy-start(f32[8]{0:T(128)S(1)} %get-tuple-element.336) | copy-start | bytes 100
  8.0 8.8 %copy-start.32 = (f32[8]{0:T(128)}, f32[8]{0:T(128)S(1)}, u32[]{:S(2)}) copy-start(f32[8]{0:T(128)S(1)} %get-tuple-element.337) | copy-start | bytes 100
  8.0 8.9 %copy-start.34 = (f32[8]{0:T(128)}, f32[8]{0:T(128)S(1)}, u32[]{:S(2)}) copy-start(f32[8]{0:T(128)S(1)} %get-tuple-element.338) | copy-start | bytes 100
  14.6 43.5 %copy-start.8 = (bf16[2,2,512,512]{3,2,1,0:T(8,128)(2,1)S(1)}, bf16[2,2,512,512]{3,2,1,0:T(8,128)(2,1)}, u32[]{:S(2)}) copy-start(bf16[2,2,512,512]{3,2,1,0:T(8,128)(2,1)} %param.26) | copy-start | bytes 6291460
  60.4 2.9 copy-start.20
  60.4 2.9 copy-start.21
  60.4 2.9 copy-start.22
  60.4 3.0 copy-start.14
  60.4 3.0 copy-start.15
  60.4 3.0 copy-start.16
  60.5 3.0 copy-start.17
  60.5 3.0 copy-start.18
  60.5 4.1 %copy-start.12 = (bf16[384,384]{1,0:T(8,128)(2,1)S(1)}, bf16[384,384]{1,0:T(8,128)(2,1)}, u32[]{:S(2)}) copy-start(bf16[384,384]{1,0:T(8,128)(2,1)} %get-tuple-element.315) | copy-start | bytes 884740
  63.3 4.0 %copy-start.10 = (bf16[512,512]{1,0:T(8,128)(2,1)S(1)}, bf16[512,512]{1,0:T(8,128)(2,1)}, u32[]{:S(2)}) copy-start(bf16[512,512]{1,0:T(8,128)(2,1)} %get-tuple-element.312) | copy-start | bytes 1572868
  84.0 1.8 copy-start.11
  87.4 7.6 %copy-start.7 = (bf16[512,512]{1,0:T(8,128)(2,1)S(1)}, bf16[512,512]{1,0:T(8,128)(2,1)}, u32[]{:S(2)}) copy-start(bf16[512,512]{1,0:T(8,128)(2,1)} %get-tuple-element.574) | copy-start | bytes 1572868 | tf_op jit(solution)/shard_map/while
  87.6 7.7 %copy-start.3 = (bf16[768,768]{1,0:T(8,128)(2,1)S(1)}, bf16[768,768]{1,0:T(8,128)(2,1)}, u32[]{:S(2)}) copy-start(bf16[768,768]{1,0:T(8,128)(2,1)} %get-tuple-element.573) | copy-start | bytes 3538948 | tf_op jit(solution)/shard_map/while
  95.3 1.8 copy-start.4
  97.7 1.9 copy-start
  97.7 1.9 copy-start.23
  97.7 1.9 copy-start.24
  97.7 1.9 copy-start.25
  102.9 1.7 copy-start.1
  104.6 212.2 %copy-start.36 = (u32[256]{0:T(256)S(1)}, u32[256]{0:T(256)}, u32[]{:S(2)}) copy-start(u32[256]{0:T(256)} %constant.174) | copy-start | bytes 3076
  104.6 214.0 %copy-start.9 = (f32[2048,128]{1,0:T(8,128)S(1)}, f32[2048,128]{1,0:T(8,128)}, u32[]{:S(2)}) copy-start(f32[2048,128]{1,0:T(8,128)} %param.24) | copy-start | bytes 3145732
  104.6 214.0 %copy-start.31 = (f32[8]{0:T(128)S(1)}, f32[8]{0:T(128)}, u32[]{:S(2)}) copy-start(f32[8]{0:T(128)} %copy-done.30) | copy-start | bytes 100
  104.6 214.0 %copy-start.33 = (f32[8]{0:T(128)S(1)}, f32[8]{0:T(128)}, u32[]{:S(2)}) copy-start(f32[8]{0:T(128)} %copy-done.32) | copy-start | bytes 100
  104.6 214.0 %copy-start.35 = (f32[8]{0:T(128)S(1)}, f32[8]{0:T(128)}, u32[]{:S(2)}) copy-start(f32[8]{0:T(128)} %copy-done.34) | copy-start | bytes 100
  (6 other events, 7.7 us)
Sparse Core Ops, SparseCore 0:
  14.8 267.9 all-reduce.4
where the time goes:
time: 332 us; the launch traced here: 330 us
  blocking collectives  247 us (74%)
  other arithmetic  27.4 us (8%)
  local copies, waits for them, and re-layouts  21.8 us (7%)
  matrix products  18.2 us (5%)
  between operations  15.6 us (5%)
    unnamed x1, blocking collectives  212 us
    all_gather x1, blocking collectives, body(): block_feats = lax.all_gather(atom_feats, 'tgt', axis=0, tiled=True)  34.9 us
    dot_general x4, matrix products, highest_dot(): jnp.dot(left_side, right_side, precision=lax.Precision.HIGHEST, preferred...  10.7 us
    concatenate x4, other arithmetic, pair_matrix(): return jnp.concatenate([upper_half, lower_half], axis=0)  9.71 us
    convert_element_type x1, other arithmetic, edge_message(): jax.nn.gelu(convolve(turned, sections[0]), approximate=False)  7.17 us
  transfers between devices with their start and end apart: 1, of which 0 were waited for; matrix products, arithmetic and copies ran while one was open for 15% of the time, Pallas kernels for 0%

commit v1 on v0

--- a/solution.py
+++ b/solution.py
@@ -92,7 +92,9 @@
                 for weights in (weight_first, weight_second, weight_third, weight_fourth)
             ]
         )
-    block_feats = lax.all_gather(atom_feats, "tgt", axis=0, tiled=True)
+    block_feats = jnp.concatenate(
+        lax.all_to_all(jnp.stack([atom_feats] * lax.axis_size("tgt")), "tgt", 0, 0), axis=0
+    )
     step_rows = math.gcd(256, capacity // 2)
     lane_ids = jnp.arange(step_rows, dtype=jnp.int32)
     target_ids = jnp.arange(target_rows, dtype=jnp.int32)

time: 332 us -> 306 us (0.922)
  blocking collectives: 247 us -> 213 us
  starting transfers between devices: 0.04 us -> 6.07 us
    all_gather x1 -> x0, blocking collectives: 34.9 us -> none  [body(): block_feats = lax.all_gather(atom_feats, 'tgt', axis=0, tiled=True)]
    all_to_all x0 -> x1, starting transfers between devices: none -> 6.03 us  [body(): lax.all_to_all(jnp.stack([atom_feats] * lax.axis_size('tgt')), 'tgt', 0, 0)]
  transfers between devices with their start and end apart: 1 -> 2, of which waited for: 0 -> 0; matrix products, arithmetic and copies ran while one was open for 15% -> 19% of each run, Pallas kernels for 0% -> 0%
where the time goes in v1:
time: 306 us; the launch traced here: 304 us
  blocking collectives  213 us (70%)
  other arithmetic  27.3 us (9%)
  local copies, waits for them, and re-layouts  23.5 us (8%)
  matrix products  18.2 us (6%)
  between operations  15.6 us (5%)
  starting transfers between devices  6.07 us (2%)
    unnamed x1, blocking collectives  213 us
    dot_general x4, matrix products, highest_dot(): jnp.dot(left_side, right_side, precision=lax.Precision.HIGHEST, preferred...  10.7 us
    concatenate x4, other arithmetic, pair_matrix(): return jnp.concatenate([upper_half, lower_half], axis=0)  9.71 us
    convert_element_type x1, other arithmetic, edge_message(): jax.nn.gelu(convolve(turned, sections[0]), approximate=False)  7.17 us
  transfers between devices with their start and end apart: 2, of which 0 were waited for; matrix products, arithmetic and copies ran while one was open for 19% of the time, Pallas kernels for 0%

profile of v1, /device:TPU:8, one launch (start us, length us, event | category | flops | bytes accessed | tf_op | source)
XLA Modules:
  0.0 304.2 jit_solution(17055466755658930581)
XLA Ops:
  7.2 1.6 stack.2
  8.8 6.0 %all-to-all-start = ((bf16[8,8,3200]{2,1,0:T(8,128)(2,1)}), bf16[8,8,3200]{2,1,0:T(8,128)(2,1)S(1)}, u32[]{:S(2)}, u32[]{:S(2)}) async-start(bf16[8,8,3200]{2,1,0:T(8,128)(2,1)} %stack.2), calls=%async_computation | async-start | bytes 819200 | tf_op jit(solution)/shard_map/all_to_all | solution.py:96
  14.9 0.8 slice_bitcast_fusion.20
  15.7 0.8 convert_element_type.28
  16.5 2.9 fusion.53
  19.4 2.9 fusion.50
  22.4 1.5 dynamic_slice.19
  25.9 0.8 slice_bitcast_fusion.10
  26.7 1.9 fusion.94
  28.6 2.3 slice_bitcast_fusion.6
  30.9 0.9 fusion.96
  31.8 1.4 slice_bitcast_fusion.2
  33.3 2.8 slice_bitcast_fusion
  37.5 1.1 maximum_maximum_fusion.4
  38.6 2.8 maximum_maximum_fusion.2
  41.4 5.8 %maximum_maximum_fusion = (bf16[1024,1024]{1,0:T(8,128)(2,1)}, bf16[1024,1024]{1,0:T(8,128)(2,1)}) fusion(bf16[512,512]{1,0:T(8,128)(2,1)} %get-tuple-element.309, bf16[512,512]{1,0:T(8,128)(2,1)S(1)} %copy-done.10, bf16[512,512]{1,0:T(8,128)(2,1)} %get-tuple-element.308, bf16[512,512]{1,0:T(8,128)(2,1)} %get-tuple-element.310, ...), kind=kLoop, calls=%fused_computation.92 | loop fusion | flops 16777216 | bytes 7340032 | tf_op jit(solution)/shard_map/concatenate | solution.py:26
  47.2 1.9 broadcast.177
  49.0 29.6 %while.13 = (s32[]{:T(128)}, f32[256,3200]{1,0:T(8,128)}, s32[]{:T(128)}, s32[1024]{0:T(1024)}, s32[1024]{0:T(1024)}, /*index=5*/bf16[64,3200]{1,0:T(8,128)(2,1)...) while((s32[]{:T(128)}, f32[256,3200]{1,0:T(8,128)}, ...), condition=%wide.region_1.2_spmd.clone.clone, body=%wide.region_0.1_spmd.clone.clone.sunk | while | flops 5013903360 | bytes 114246840 | solution.py:137
  49.0 1.3 dynamic_slice.35
  50.4 1.3 dynamic_slice.36
  51.7 2.0 compare_and_fusion.2
  53.7 0.8 broadcast_multiply_fusion.7
  55.2 1.8 gather_fusion
  57.0 1.1 fusion.157
  59.9 0.7 convolution_dynamic-update-slice_fusion.13
  61.7 7.2 %fusion.158 = bf16[256,3200]{1,0:T(8,128)(2,1)S(1)} fusion(f32[256,3200]{1,0:T(8,128)S(1)} %convolution_dynamic-update-slice_fusion.16), kind=kLoop, calls=%fused_computation.6.clone.1 | loop fusion | flops 53248000 | bytes 4915200 | tf_op jit(solution)/shard_map/while/body/convert_element_type | solution.py:106
  72.8 0.9 copy-done
  73.7 3.3 %convolution_add_fusion.3 = f32[256,3200]{1,0:T(8,128)S(1)} fusion(f32[256,3200]{1,0:T(8,128)S(1)} %copy-done, f32[256,3200]{1,0:T(8,128)S(1)} %subtract_dynamic-update-slice_fusion.11, f32[256]{0:T(256)S(1)} %copy-done.23, f32[256]{0:T(256)S(1)} %copy-done.24, s32[256]{0:T(256)S(1)} %copy-done.25), kind=kOutput, calls=%fused_computation.2.clone.1 | convolution fusion | flops 2519105536 | bytes 9833472 | tf_op jit(solution)/shard_map/while/body/dot_general | solution.py:128
  77.0 1.6 copy-done.1
  78.7 213.1 %all-reduce.6 = bf16[256,3200]{1,0:T(8,128)(2,1)S(1)} all-reduce(f32[256,3200]{1,0:T(8,128)} %get-tuple-element.155), channel_id=2, replica_groups=mesh['src'=32,'tgt'=8] {'src'}, use_global_device_ids=true, to_apply=%region_2.3.clone | all-reduce | flops 819200 | bytes 4915200
  292.4 2.1 fusion.45
  294.6 2.8 fusion.43
  (105 shorter events, 9.9 us)
Async XLA Ops:
  7.2 17.4 %copy-start.19 = (bf16[2,2,128,128]{3,2,1,0:T(8,128)(2,1)S(1)}, bf16[2,2,128,128]{3,2,1,0:T(8,128)(2,1)}, u32[]{:S(2)}) copy-start(bf16[2,2,128,128]{3,2,1,0:T(8,128)(2,1)} %param.29) | copy-start | bytes 393220
  7.2 18.0 %copy-start.13 = (bf16[2,2,256,256]{3,2,1,0:T(8,128)(2,1)S(1)}, bf16[2,2,256,256]{3,2,1,0:T(8,128)(2,1)}, u32[]{:S(2)}) copy-start(bf16[2,2,256,256]{3,2,1,0:T(8,128)(2,1)} %param.28) | copy-start | bytes 1572868
  8.8 38.3 %all-to-all-start = ((bf16[8,8,3200]{2,1,0:T(8,128)(2,1)}), bf16[8,8,3200]{2,1,0:T(8,128)(2,1)S(1)}, u32[]{:S(2)}, u32[]{:S(2)}) async-start(bf16[8,8,3200]{2,1,0:T(8,128)(2,1)} %stack.2), calls=%async_computation | async-start | bytes 819200 | tf_op jit(solution)/shard_map/all_to_all | solution.py:96
  14.9 277.5 %all-reduce.5.cloned.1.call-start = ((), (), s32[]{:S(2)}) async-start(), calls=%async_computation.1 | async-start | bytes 4194304 | tf_op jit(solution)/shard_map/psum | solution.py:147
  15.7 8.8 %copy-start.29 = (f32[8]{0:T(128)}, f32[8]{0:T(128)S(1)}, u32[]{:S(2)}) copy-start(f32[8]{0:T(128)S(1)} %get-tuple-element.336) | copy-start | bytes 100
  15.7 8.8 %copy-start.31 = (f32[8]{0:T(128)}, f32[8]{0:T(128)S(1)}, u32[]{:S(2)}) copy-start(f32[8]{0:T(128)S(1)} %get-tuple-element.337) | copy-start | bytes 100
  15.7 8.8 %copy-start.33 = (f32[8]{0:T(128)}, f32[8]{0:T(128)S(1)}, u32[]{:S(2)}) copy-start(f32[8]{0:T(128)S(1)} %get-tuple-element.338) | copy-start | bytes 100
  22.3 8.6 %copy-start.8 = (bf16[2,2,512,512]{3,2,1,0:T(8,128)(2,1)S(1)}, bf16[2,2,512,512]{3,2,1,0:T(8,128)(2,1)}, u32[]{:S(2)}) copy-start(bf16[2,2,512,512]{3,2,1,0:T(8,128)(2,1)} %param.26) | copy-start | bytes 6291460
  31.8 4.3 %copy-start.35 = (u32[256]{0:T(256)S(1)}, u32[256]{0:T(256)}, u32[]{:S(2)}) copy-start(u32[256]{0:T(256)} %constant.174) | copy-start | bytes 3076
  33.2 4.2 %copy-start.20 = (bf16[128,128]{1,0:T(8,128)(2,1)S(1)}, bf16[128,128]{1,0:T(8,128)(2,1)}, u32[]{:S(2)}) copy-start(bf16[128,128]{1,0:T(8,128)(2,1)} %get-tuple-element.328) | copy-start | bytes 98308
  33.2 4.2 %copy-start.21 = (bf16[128,128]{1,0:T(8,128)(2,1)S(1)}, bf16[128,128]{1,0:T(8,128)(2,1)}, u32[]{:S(2)}) copy-start(bf16[128,128]{1,0:T(8,128)(2,1)} %get-tuple-element.329) | copy-start | bytes 98308
  33.2 4.2 %copy-start.22 = (bf16[128,128]{1,0:T(8,128)(2,1)S(1)}, bf16[128,128]{1,0:T(8,128)(2,1)}, u32[]{:S(2)}) copy-start(bf16[128,128]{1,0:T(8,128)(2,1)} %get-tuple-element.330) | copy-start | bytes 98308
  33.2 4.2 %copy-start.14 = (bf16[256,256]{1,0:T(8,128)(2,1)S(1)}, bf16[256,256]{1,0:T(8,128)(2,1)}, u32[]{:S(2)}) copy-start(bf16[256,256]{1,0:T(8,128)(2,1)} %get-tuple-element.326) | copy-start | bytes 393220
  33.2 4.2 %copy-start.15 = (bf16[256,256]{1,0:T(8,128)(2,1)S(1)}, bf16[256,256]{1,0:T(8,128)(2,1)}, u32[]{:S(2)}) copy-start(bf16[256,256]{1,0:T(8,128)(2,1)} %get-tuple-element.321) | copy-start | bytes 393220
  33.2 4.2 %copy-start.16 = (bf16[256,256]{1,0:T(8,128)(2,1)S(1)}, bf16[256,256]{1,0:T(8,128)(2,1)}, u32[]{:S(2)}) copy-start(bf16[256,256]{1,0:T(8,128)(2,1)} %get-tuple-element.322) | copy-start | bytes 393220
  33.2 4.2 %copy-start.17 = (bf16[256,256]{1,0:T(8,128)(2,1)S(1)}, bf16[256,256]{1,0:T(8,128)(2,1)}, u32[]{:S(2)}) copy-start(bf16[256,256]{1,0:T(8,128)(2,1)} %get-tuple-element.323) | copy-start | bytes 393220
  33.2 4.2 %copy-start.18 = (bf16[256,256]{1,0:T(8,128)(2,1)S(1)}, bf16[256,256]{1,0:T(8,128)(2,1)}, u32[]{:S(2)}) copy-start(bf16[256,256]{1,0:T(8,128)(2,1)} %get-tuple-element.324) | copy-start | bytes 393220
  33.2 5.3 %copy-start.12 = (bf16[384,384]{1,0:T(8,128)(2,1)S(1)}, bf16[384,384]{1,0:T(8,128)(2,1)}, u32[]{:S(2)}) copy-start(bf16[384,384]{1,0:T(8,128)(2,1)} %get-tuple-element.315) | copy-start | bytes 884740
  36.1 5.3 %copy-start.10 = (bf16[512,512]{1,0:T(8,128)(2,1)S(1)}, bf16[512,512]{1,0:T(8,128)(2,1)}, u32[]{:S(2)}) copy-start(bf16[512,512]{1,0:T(8,128)(2,1)} %get-tuple-element.312) | copy-start | bytes 1572868
  58.1 1.9 copy-start.11
  61.5 7.6 %copy-start.7 = (bf16[512,512]{1,0:T(8,128)(2,1)S(1)}, bf16[512,512]{1,0:T(8,128)(2,1)}, u32[]{:S(2)}) copy-start(bf16[512,512]{1,0:T(8,128)(2,1)} %get-tuple-element.574) | copy-start | bytes 1572868 | tf_op jit(solution)/shard_map/while
  61.7 7.7 %copy-start.3 = (bf16[768,768]{1,0:T(8,128)(2,1)S(1)}, bf16[768,768]{1,0:T(8,128)(2,1)}, u32[]{:S(2)}) copy-start(bf16[768,768]{1,0:T(8,128)(2,1)} %get-tuple-element.573) | copy-start | bytes 3538948 | tf_op jit(solution)/shard_map/while
  69.4 1.8 copy-start.4
  71.8 1.9 copy-start
  71.8 1.9 copy-start.23
  71.8 1.9 copy-start.24
  71.8 1.9 copy-start.25
  77.0 1.7 copy-start.1
  78.7 213.7 %copy-start.9 = (f32[2048,128]{1,0:T(8,128)S(1)}, f32[2048,128]{1,0:T(8,128)}, u32[]{:S(2)}) copy-start(f32[2048,128]{1,0:T(8,128)} %param.24) | copy-start | bytes 3145732
  78.7 213.7 %copy-start.30 = (f32[8]{0:T(128)S(1)}, f32[8]{0:T(128)}, u32[]{:S(2)}) copy-start(f32[8]{0:T(128)} %copy-done.29) | copy-start | bytes 100
  78.7 213.7 %copy-start.32 = (f32[8]{0:T(128)S(1)}, f32[8]{0:T(128)}, u32[]{:S(2)}) copy-start(f32[8]{0:T(128)} %copy-done.31) | copy-start | bytes 100
  78.7 213.7 %copy-start.34 = (f32[8]{0:T(128)S(1)}, f32[8]{0:T(128)}, u32[]{:S(2)}) copy-start(f32[8]{0:T(128)} %copy-done.33) | copy-start | bytes 100
  (6 other events, 7.8 us)
Sparse Core Ops, SparseCore 0:
  22.4 268.8 all-reduce.4
